TPU v7x, 32 devices: a whole 2x2x4 slice. The times are simulated.
32 devices in a mesh: depth: 4 (over y, core), hx: 4 (over z), hy: 2 (over x).
Axes of the slice: x: 2, y: 2, z: 4, core: 2. Of those that a mesh axis runs over, the one named last changes fastest.
Arguments:
- fine_velocity: float32 [3, 16, 24, 768], P(None, 'depth', 'hx', 'hy'), may hold values from -6 to 6
- fine_stress: float32 [6, 16, 24, 768], P(None, 'depth', 'hx', 'hy'), may hold values from -3 to 3
- coarse_velocity: float32 [3, 8, 8, 256], P(None, 'depth', 'hx', 'hy'), may hold values from -6 to 6
- coarse_stress: float32 [6, 8, 8, 256], P(None, 'depth', 'hx', 'hy'), may hold values from -3 to 3
- iwan_states: float32 [10, 6, 16, 24, 768], P(None, None, 'depth', 'hx', 'hy'), may hold values from -0.3 to 0.3
- fine_zones: int32 [16, 24, 768], P('depth', 'hx', 'hy'), may hold values from 0 to 15
- coarse_zones: int32 [8, 8, 256], P('depth', 'hx', 'hy'), may hold values from 0 to 15
- plastic: int32 [16, 24, 768], P('depth', 'hx', 'hy'), may hold values from 0 to 1, as said below
- zone_buoyancy: float32 [16], replicated, may hold values from 0.5 to 1
- zone_lambda: float32 [16], replicated, may hold values from 0.1 to 0.3
- zone_mu: float32 [16], replicated, may hold values from 0.1 to 0.3
- iwan_share: float32 [10], replicated, may hold values from 0.3 to 3
- iwan_radius: float32 [10], replicated, may hold values from 0.01 to 0.3
Outputs:
- fine_velocity_out: float32 [3, 16, 24, 768], P(None, 'depth', 'hx', 'hy')
- fine_stress_out: float32 [6, 16, 24, 768], P(None, 'depth', 'hx', 'hy')
- coarse_velocity_out: float32 [3, 8, 8, 256], P(None, 'depth', 'hx', 'hy')
- coarse_stress_out: float32 [6, 8, 8, 256], P(None, 'depth', 'hx', 'hy')
Inputs may be any that keep to these rules, and one draw needn't show every extreme that they name: `plastic`: 1 marks a cell that follows the Iwan model, 0 an elastic cell.
All inputs are finite; a program needn't handle non-finite values.
Results may differ from a plain program's by a relative error of at most 0.0001.
Values sent between devices are 32-bit elements; how exact they have to be, the bound alone decides.
A program may use at most 64 MiB of HBM per device.

v0:
```python
import jax
import jax.numpy as jnp
from jax import lax
from jax.experimental import pallas as pl
from jax.experimental.pallas import tpu as pltpu
from jax.sharding import PartitionSpec as P

STEPS = 2
DT = 0.4
NEAR = 9.0 / 8.0
FAR = 1.0 / 24.0
MESH = pl.DeviceIdType.MESH
Z_PARTS, X_PARTS, Y_PARTS = (2, 4, 5), (0, 3, 4), (1, 3, 5)
AXES = ("depth", "hx", "hy")


class Grid:
    def __init__(self, shape, spacing, flipped):
        self.nz, self.nx, self.ny = shape
        self.near, self.far = NEAR / spacing, FAR / spacing
        self.flipped = flipped

    def at(self, z):
        return self.nz - 1 - z if self.flipped else z


def roll(x, amount, axis):
    return pltpu.roll(x, amount % x.shape[axis], axis)


def diff_z(g, ref, c, z, forward):
    o = 2 + z + (1 if forward else 0)
    return g.near * (ref[c, o] - ref[c, o - 1]) - g.far * (ref[c, o + 1] - ref[c, o - 2])


def diff_x(g, ref, c, z, forward):
    o = 3 if forward else 2
    at = lambda s: ref[c, z, s : s + g.nx, :]
    return g.near * (at(o) - at(o - 1)) - g.far * (at(o + 1) - at(o - 2))


def diff_y(g, ref, c, z, forward):
    ext = ref[c, z]
    at = lambda s: (roll(ext, -s, 1) if s else ext)[:, : g.ny]
    o = 1 if forward else 0
    return g.near * (at(o) - at(o - 1)) - g.far * (at(o + 1) - at(o - 2))


def put_ext(g, ext, comps, z, values):
    ze, xe, ye = ext
    zc, xc, yc = comps
    for slot, c in enumerate(zc):
        ze[slot, 2 + z] = values[c]
    for slot, c in enumerate(xc):
        xe[slot, z, 2 : 2 + g.nx, :] = values[c]
    for slot, c in enumerate(yc):
        ye[slot, z, :, : g.ny] = values[c]


def pack(fine, coarse, fext, cext, sz, sx, sy):
    fz, fx, fy = fext
    cz, cx, cy = cext
    for c in range(3):
        for l in range(2):
            for side in range(2):
                fl = l if side == 0 else fine.nz - 2 + l
                cl = l if side == 1 else coarse.nz - 2 + l
                sz[side, 2 * c + l, 0 : fine.nx, :] = fz[c, 2 + fl]
                sz[side, 2 * c + l, fine.nx : fine.nx + coarse.nx, 0 : coarse.ny] = cz[c, 2 + cl]
        for g, ext in ((fine, fx), (coarse, cx)):
            for z in range(g.nz):
                for side in range(2):
                    first = 2 if side == 0 else g.nx
                    rows = ext[c, z, first : first + 2, :]
                    if g is fine:
                        sx[side, c, 2 * z : 2 * z + 2, :] = rows
                    else:
                        sx[side, 3, 2 * z : 2 * z + 2, c * g.ny : (c + 1) * g.ny] = rows
    for tile, (g, ext) in enumerate(((fine, fy), (coarse, cy))):
        lane = lax.broadcasted_iota(jnp.int32, (g.nx, 128), 1)
        total = jnp.zeros((g.nx, 128), jnp.float32)
        for c in range(3):
            for z in range(g.nz):
                i = c * g.nz + z
                plane = ext[c, z, :, 0:128]
                if g.ny > 128:
                    plane = jnp.where(lane < 64, plane, ext[c, z, :, g.ny - 128 : g.ny])
                total = jnp.where(lane // 4 == i, roll(plane, 4 * i + 2, 1), total)
        sy[tile, 0 : g.nx, :] = total


def unpack_z(fine, coarse, fext, cext, rz):
    for c in range(3):
        for l in range(2):
            for side in range(2):
                fext[0][c, l if side == 0 else 2 + fine.nz + l] = rz[side, 2 * c + l, 0 : fine.nx, :]
                cext[0][c, l if side == 1 else 2 + coarse.nz + l] = rz[
                    side, 2 * c + l, fine.nx : fine.nx + coarse.nx, 0 : coarse.ny
                ]


def unpack_x(fine, coarse, fext, cext, rx):
    for c in range(3):
        for g, ext in ((fine, fext[1]), (coarse, cext[1])):
            for z in range(g.nz):
                for side in range(2):
                    first = 0 if side == 0 else 2 + g.nx
                    if g is fine:
                        rows = rx[side, c, 2 * z : 2 * z + 2, :]
                    else:
                        rows = rx[side, 3, 2 * z : 2 * z + 2, c * g.ny : (c + 1) * g.ny]
                    ext[c, z, first : first + 2, :] = rows


def unpack_y(fine, coarse, fext, cext, ry):
    for tile, (g, ext) in enumerate(((fine, fext[2]), (coarse, cext[2]))):
        lane = lax.broadcasted_iota(jnp.int32, (g.nx, 128), 1)
        both = jnp.where(lane % 4 < 2, ry[0, tile, 0 : g.nx, :], ry[1, tile, 0 : g.nx, :])
        for c in range(3):
            for z in range(g.nz):
                i = c * g.nz + z
                ext[c, z, :, g.ny : g.ny + 128] = roll(both, -(4 * i + 2), 1)


def couple(fine, coarse, fext, cext):
    fz, cz = fext[0], cext[0]
    nt = fine.ny // 128
    lane = lax.broadcasted_iota(jnp.int32, (fine.nx, 128), 1)
    row = lax.broadcasted_iota(jnp.int32, (fine.nx, 128), 0)
    clane = lane[0 : coarse.nx]
    ratio = fine.ny // coarse.ny
    for c in range(3):
        bottom = fz[c, 1 + fine.nz]
        plane = cz[c, 2]
        rows = jnp.broadcast_to(plane[0:1], (fine.nx, coarse.ny))
        for r in range(1, coarse.nx):
            rows = jnp.where(row < 3 * r, rows, jnp.broadcast_to(plane[r : r + 1], rows.shape))
        spread = jnp.concatenate(
            [jnp.take_along_axis(rows, (lane + 128 * t) // 3, axis=1) for t in range(nt)], axis=1
        )
        fz[c, 2 + fine.nz] = 2.0 / 3.0 * bottom + 1.0 / 3.0 * spread
        fz[c, 3 + fine.nz] = 1.0 / 3.0 * bottom + 2.0 / 3.0 * spread
        for slot, z in ((1, fine.nz - 1), (0, fine.nz - 4)):
            f = fz[c, 2 + z]
            f = f + roll(f, -1, 1) + roll(f, -2, 1)
            sums = jnp.concatenate(
                [jnp.sum(f[3 * r : 3 * r + 3], axis=0, keepdims=True) for r in range(coarse.nx)], axis=0
            )
            out = jnp.zeros((coarse.nx, 128), jnp.float32)
            for t in range(nt):
                got = jnp.take_along_axis(sums[:, 128 * t : 128 * t + 128], (3 * clane) % 128, axis=1)
                out = jnp.where((3 * clane) // 128 == t, got, out)
            cz[c, slot] = out * (1.0 / 9.0)


def materials(g, zones, tables, out):
    def body(z, carry):
        ids = zones[g.at(z)]
        values = [jnp.zeros(ids.shape, jnp.float32)] * 3
        for member in range(tables[0].shape[0]):
            hit = ids == member
            values = [jnp.where(hit, t[member], v) for t, v in zip(tables, values)]
        out[0, z] = DT * values[0]
        out[1, z] = DT * values[1]
        out[2, z] = DT * values[2]
        return carry

    lax.fori_loop(0, g.nz, body, 0)


def velocity_update(g, sext, vext, mats, velocity):
    ze, xe, ye = sext
    allc = (0, 1, 2)

    def body(z, carry):
        b = mats[0, z]
        force = (
            diff_x(g, xe, 0, z, True) + diff_y(g, ye, 1, z, False) + diff_z(g, ze, 1, z, False),
            diff_x(g, xe, 1, z, False) + diff_y(g, ye, 0, z, True) + diff_z(g, ze, 2, z, False),
            diff_x(g, xe, 2, z, False) + diff_y(g, ye, 2, z, False) + diff_z(g, ze, 0, z, True),
        )
        new = [velocity[c, g.at(z)] + b * force[c] for c in range(3)]
        for c in range(3):
            velocity[c, g.at(z)] = new[c]
        put_ext(g, vext, (allc, allc, allc), z, new)
        return carry

    lax.fori_loop(0, g.nz, body, 0)


def stress_update(g, vext, sext, mats, stress, iwan, last):
    ze, xe, ye = vext

    def body(z, carry):
        lame, shear = mats[1, z], mats[2, z]
        exx = diff_x(g, xe, 0, z, False)
        eyy = diff_y(g, ye, 1, z, False)
        ezz = diff_z(g, ze, 2, z, False)
        exy = diff_x(g, xe, 1, z, True) + diff_y(g, ye, 0, z, True)
        exz = diff_x(g, xe, 2, z, True) + diff_z(g, ze, 0, z, True)
        eyz = diff_y(g, ye, 2, z, True) + diff_z(g, ze, 1, z, True)
        dilation = exx + eyy + ezz
        old = [stress[c, g.at(z)] for c in range(6)]
        volume = lame * dilation
        twice = 2.0 * shear
        shears = [shear * exy, shear * exz, shear * eyz]
        new = [old[c] + volume + twice * e for c, e in enumerate((exx, eyy, ezz))]
        new += [old[3 + c] + shears[c] for c in range(3)]
        if iwan is not None:
            states, plastic, share, radius, surfaces = iwan
            third = dilation * (1.0 / 3.0)
            total = share[0]
            for k in range(1, surfaces):
                total = total + share[k]
            scale = 1.0 / jnp.full(dilation.shape, total, jnp.float32)
            dd = [scale * (twice * (e - third)) for e in (exx, eyy, ezz)]
            dd += [scale * s for s in shears]
            sums = None
            for k in range(surfaces):
                t = [states[k, c, z] + share[k] * dd[c] for c in range(6)]
                j2 = 0.5 * (t[0] * t[0] + t[1] * t[1] + t[2] * t[2]) + (
                    t[3] * t[3] + t[4] * t[4] + t[5] * t[5]
                )
                factor = jnp.minimum(1.0, radius[k] * lax.rsqrt(j2))
                t = [factor * x for x in t]
                if not last:
                    for c in range(6):
                        states[k, c, z] = t[c]
                sums = t if sums is None else [a + b for a, b in zip(sums, t)]
            mean = (old[0] + old[1] + old[2]) * (1.0 / 3.0) + (lame + twice * (1.0 / 3.0)) * dilation
            active = plastic[z] == 1
            yielded = [mean + sums[c] for c in range(3)] + sums[3:]
            new = [jnp.where(active, a, b) for a, b in zip(yielded, new)]
        for c in range(6):
            stress[c, g.at(z)] = new[c]
        if not last:
            put_ext(g, sext, (Z_PARTS, X_PARTS, Y_PARTS), z, new)
        return carry

    lax.fori_loop(0, g.nz, body, 0)


def kernel(counts, fine, coarse, surfaces, *refs):
    (fv_in, fs_in, cv_in, cs_in, st_in, fzo_in, czo_in, pl_in) = refs[:8]
    tables, share, radius = refs[8:11], refs[11], refs[12]
    fv_out, fs_out, cv_out, cs_out = refs[13:17]
    (fv, fs, cv, cs, st, fzo, czo, plastic) = refs[17:25]
    fmat, cmat = refs[25:27]
    fsx, csx, fvx, cvx = refs[27:30], refs[30:33], refs[33:36], refs[36:39]
    sends, recvs = refs[39:42], refs[42:45]
    in_sem, out_sem, send_sem, recv_sem = refs[45:49]

    place = [lax.axis_index(a) for a in AXES]
    exists = lambda a, side: (place[a] > 0) if side == 0 else (place[a] < counts[a] - 1)
    peer = lambda a, side: {AXES[a]: place[a] + (1 if side else -1)}

    order = (1, 3, 0, 2, 5, 6, 7, 4)
    loads = [
        pltpu.make_async_copy(src, dst, in_sem.at[i])
        for i, (src, dst) in enumerate(zip(refs[:8], refs[17:25]))
    ]
    for i in order:
        loads[i].start()

    barrier = pltpu.get_barrier_semaphore()
    for a in range(3):
        for side in range(2):

            @pl.when(exists(a, side))
            def _():
                pl.semaphore_signal(barrier, inc=1, device_id=peer(a, side), device_id_type=MESH)

            @pl.when(jnp.logical_not(exists(a, side)))
            def _():
                for e in range(2 * STEPS):
                    recvs[a][e, side] = jnp.zeros(recvs[a].shape[2:], jnp.float32)

    def copy(e, a, side):
        src = sends[a].at[e, side] if a < 2 else sends[a].at[e]
        return pltpu.make_async_remote_copy(
            src_ref=src,
            dst_ref=recvs[a].at[e, 1 - side],
            send_sem=send_sem.at[e, a, side],
            recv_sem=recv_sem.at[e, a, 1 - side],
            device_id=peer(a, side),
            device_id_type=MESH,
        )

    def start(e):
        for a in range(3):
            for side in range(2):

                @pl.when(exists(a, side))
                def _():
                    copy(e, a, side).start()

    def arrive(e, a):
        for side in range(2):

            @pl.when(exists(a, side))
            def _():
                copy(e, a, 1 - side).wait_recv()

    loads[1].wait()
    loads[3].wait()
    for g, s, ext in ((fine, fs, fsx), (coarse, cs, csx)):
        for z in range(g.nz):
            put_ext(g, ext, (Z_PARTS, X_PARTS, Y_PARTS), z, [s[c, g.at(z)] for c in range(6)])

    at_interface = place[0] == counts[0] - 1
    for e in range(2 * STEPS):
        fext, cext = (fsx, csx) if e % 2 == 0 else (fvx, cvx)
        pack(fine, coarse, fext, cext, sends[0].at[e], sends[1].at[e], sends[2].at[e])
        if e == 0:
            neighbours = sum(
                exists(a, side).astype(jnp.int32) for a in range(3) for side in range(2)
            )
            pl.semaphore_wait(barrier, neighbours)
        start(e)
        if e == 0:
            loads[5].wait()
            loads[6].wait()
            materials(fine, fzo, tables, fmat)
            materials(coarse, czo, tables, cmat)
            loads[0].wait()
            loads[2].wait()
        arrive(e, 2)
        unpack_y(fine, coarse, fext, cext, recvs[2].at[e])
        arrive(e, 0)
        unpack_z(fine, coarse, fext, cext, recvs[0].at[e])

        @pl.when(at_interface)
        def _():
            couple(fine, coarse, fext, cext)

        arrive(e, 1)
        unpack_x(fine, coarse, fext, cext, recvs[1].at[e])
        last = e >= 2 * STEPS - 2
        if e % 2 == 0:
            velocity_update(fine, fsx, fvx, fmat, fv)
            velocity_update(coarse, csx, cvx, cmat, cv)
            if last:
                stores = [
                    pltpu.make_async_copy(fv, fv_out, out_sem.at[0]),
                    pltpu.make_async_copy(cv, cv_out, out_sem.at[1]),
                ]
                for s in stores:
                    s.start()
        else:
            if e == 1:
                loads[7].wait()
                loads[4].wait()
            stress_update(
                fine, fvx, fsx, fmat, fs, (st, plastic, share, radius, surfaces), last
            )
            stress_update(coarse, cvx, csx, cmat, cs, None, last)
    tail = [
        pltpu.make_async_copy(fs, fs_out, out_sem.at[2]),
        pltpu.make_async_copy(cs, cs_out, out_sem.at[3]),
    ]
    for s in tail:
        s.start()
    for e in range(2 * STEPS):
        for a in range(3):
            for side in range(2):

                @pl.when(exists(a, side))
                def _():
                    copy(e, a, side).wait_send()

    for s in stores + tail:
        s.wait()


def per_device(counts, *args):
    fv, fs, cv, cs, st = args[:5]
    fine = Grid(fv.shape[1:], 1.0, False)
    coarse = Grid(cv.shape[1:], 3.0, True)
    f32 = jnp.float32

    def exts(g):
        return [
            pltpu.VMEM((3, g.nz + 4, g.nx, g.ny), f32),
            pltpu.VMEM((3, g.nz, -(-(g.nx + 4) // 8) * 8, g.ny), f32),
            pltpu.VMEM((3, g.nz, g.nx, g.ny + 128), f32),
        ]

    zrows = -(-(fine.nx + coarse.nx) // 8) * 8
    xrows = -(-2 * max(fine.nz, coarse.nz) // 8) * 8
    shapes = ((6, zrows, fine.ny), (4, xrows, fine.ny), (2, 8, 128))
    phases = 2 * STEPS
    scratch = [pltpu.VMEM(a.shape, a.dtype) for a in args[:8]]
    scratch += [pltpu.VMEM((3, g.nz, g.nx, g.ny), f32) for g in (fine, coarse)]
    scratch += exts(fine) + exts(coarse) + exts(fine) + exts(coarse)
    scratch += [
        pltpu.VMEM((phases, 2) + shapes[0], f32),
        pltpu.VMEM((phases, 2) + shapes[1], f32),
        pltpu.VMEM((phases,) + shapes[2], f32),
    ]
    scratch += [pltpu.VMEM((phases, 2) + s, f32) for s in shapes]
    scratch += [
        pltpu.SemaphoreType.DMA((8,)),
        pltpu.SemaphoreType.DMA((4,)),
        pltpu.SemaphoreType.DMA((phases, 3, 2)),
        pltpu.SemaphoreType.DMA((phases, 3, 2)),
    ]
    anywhere = pl.BlockSpec(memory_space=pl.ANY)
    scalars = pl.BlockSpec(memory_space=pltpu.SMEM)
    return pl.pallas_call(
        lambda *refs: kernel(counts, fine, coarse, st.shape[0], *refs),
        name="waves",
        out_shape=[jax.ShapeDtypeStruct(a.shape, a.dtype) for a in (fv, fs, cv, cs)],
        in_specs=[anywhere] * 8 + [scalars] * 5,
        out_specs=[anywhere] * 4,
        scratch_shapes=scratch,
        compiler_params=pltpu.CompilerParams(collective_id=0, has_side_effects=True),
    )(*args)


def solution(mesh):
    field = P(None, *AXES)
    cells = P(*AXES)
    counts = tuple(mesh.shape[a] for a in AXES)
    return jax.shard_map(
        lambda *args: tuple(per_device(counts, *args)),
        mesh=mesh,
        in_specs=(field,) * 4 + (P(None, None, *AXES),) + (cells,) * 3 + (P(),) * 5,
        out_specs=(field,) * 4,
        check_vma=False,
    )
```

profile of v0, /device:TPU:0, one launch (start us, length us, event | category | flops | bytes accessed | tf_op | source)
XLA Modules:
  0.0 40.1 jit_solution(15571195694505091245)
XLA Ops:
  0.6 1.4 %copy.20.refs_5_ = s32[4,6,384]{2,1,0:T(8,128)} copy(s32[4,6,384]{2,0,1:T(4,128)} %param.18) | data formatting | bytes 73728 | tf_op args[5]
  2.0 1.4 %copy.21.refs_7_ = s32[4,6,384]{2,1,0:T(8,128)} copy(s32[4,6,384]{2,0,1:T(4,128)} %param.20) | data formatting | bytes 73728 | tf_op args[7]
  3.4 1.6 %copy.17.refs_0_ = f32[3,4,6,384]{3,2,1,0:T(8,128)} copy(f32[3,4,6,384]{3,1,2,0:T(4,128)} %param.13) | data formatting | bytes 221184 | tf_op args[0]
  5.0 1.7 %copy.18.refs_1_ = f32[6,4,6,384]{3,2,1,0:T(8,128)} copy(f32[6,4,6,384]{3,1,2,0:T(4,128)} %param.14) | data formatting | bytes 442368 | tf_op args[1]
  6.7 3.7 %copy.19.refs_4_ = f32[10,6,4,6,384]{4,3,2,1,0:T(8,128)} copy(f32[10,6,4,6,384]{4,2,3,1,0:T(4,128)} %param.17) | data formatting | bytes 4423680 | tf_op args[4]
  10.4 23.9 %waves.1 = (f32[3,4,6,384]{3,2,1,0:T(8,128)}, f32[6,4,6,384]{3,2,1,0:T(8,128)}, f32[3,2,2,128]{3,2,1,0:T(2,128)}, f32[6,2,2,128]{3,2,1,0:T(2,128)}) custom-call(f32[3,4,6,384]{3,2,1,0:T(8,128)} %copy.17.refs_0_, f32[6,4,6,384]{3,2,1,0:T(8,128)} %copy.18.refs_1_, f32[3,2,2,128]{3,2,1,0:T(2,128)} %refs_2_.1, f32[6,2,2,128]{3,2,1,0:T(2,128)} %refs_3_.1, ...), custom_call_target="tpu_custom_call" | custom-call | tf_op jit(solution)/shard_map/waves/pallas_call | solution.py:409
  34.3 1.6 %copy.22 = f32[3,4,6,384]{3,1,2,0:T(4,128)} copy(f32[3,4,6,384]{3,2,1,0:T(8,128)} %get-tuple-element.4) | data formatting | bytes 221184 | tf_op jit(solution)/shard_map/waves/pallas_call | solution.py:409
  35.8 1.7 %copy.23 = f32[6,4,6,384]{3,1,2,0:T(4,128)} copy(f32[6,4,6,384]{3,2,1,0:T(8,128)} %get-tuple-element.5) | data formatting | bytes 442368 | tf_op jit(solution)/shard_map/waves/pallas_call | solution.py:409
  37.6 1.3 %copy.26 = f32[3,2,2,128]{3,2,1,0:T(2,128)} copy(f32[3,2,2,128]{3,2,1,0:T(2,128)} %get-tuple-element.14) | data formatting | bytes 12288
  38.8 1.3 %copy.27 = f32[6,2,2,128]{3,2,1,0:T(2,128)} copy(f32[6,2,2,128]{3,2,1,0:T(2,128)} %get-tuple-element.15) | data formatting | bytes 24576
where the time goes:
time: 40.6 us; the launch traced here: 40.1 us
  Pallas kernels  23.9 us (59%)
  local copies, waits for them, and re-layouts  15.6 us (38%)
  between operations  0.64 us (2%)
    pallas_call x1, Pallas kernels, per_device(): pl.pallas_call(lambda *refs: kernel(counts, fine, coarse, st.shape[0], *r...  23.9 us
    unnamed x7, local copies, waits for them, and re-layouts  12.4 us
    pallas_call x2, local copies, waits for them, and re-layouts, per_device(): pl.pallas_call(lambda *refs: kernel(counts, fine, coarse, st.shape[0], *r...  3.29 us

commit v1 on v0

v1 whole, which is shorter than its diff:
```python
import jax
import jax.numpy as jnp
from jax import lax
from jax.experimental import pallas as pl
from jax.experimental.pallas import tpu as pltpu
from jax.sharding import PartitionSpec as P

STEPS = 2
DT = 0.4
NEAR = 9.0 / 8.0
FAR = 1.0 / 24.0
MESH = pl.DeviceIdType.MESH
Z_PARTS, X_PARTS, Y_PARTS = (2, 4, 5), (0, 3, 4), (1, 3, 5)
AXES = ("depth", "hx", "hy")


class Grid:
    def __init__(self, shape, spacing, flipped, lead):
        self.lead, self.sub, self.ny = shape
        self.near, self.far = NEAR / spacing, FAR / spacing
        self.flipped = flipped
        self.lead_axis = lead

    def at(self, n):
        return self.lead - 1 - n if self.flipped else n


def roll(x, amount, axis):
    return pltpu.roll(x, amount % x.shape[axis], axis)


def diff(g, axis, ext, c, n, forward):
    ref = ext[axis]
    if axis == 2:
        full = ref[c, n]
        at = lambda s: (roll(full, -s, 1) if s else full)[:, : g.ny]
        o = 0
    elif axis == g.lead_axis:
        at = lambda s: ref[c, s]
        o = 2 + n
    else:
        at = lambda s: ref[c, n, s : s + g.sub, :]
        o = 2
    o = o + 1 if forward else o
    return g.near * (at(o) - at(o - 1)) - g.far * (at(o + 1) - at(o - 2))


def put_ext(g, ext, comps, n, values):
    for axis in range(3):
        for slot, c in enumerate(comps[axis]):
            if axis == 2:
                ext[axis][slot, n, :, : g.ny] = values[c]
            elif axis == g.lead_axis:
                ext[axis][slot, 2 + n] = values[c]
            else:
                ext[axis][slot, n, 2 : 2 + g.sub, :] = values[c]


def pack_sub(g, ext, out):
    ref = ext[1 - g.lead_axis]
    for c in range(3):
        for n in range(g.lead):
            out[0, c, n] = ref[c, n, 2:4, :]
            out[1, c, n] = ref[c, n, g.sub : g.sub + 2, :]


def unpack_sub(g, ext, got):
    ref = ext[1 - g.lead_axis]
    for c in range(3):
        for n in range(g.lead):
            ref[c, n, 0:2, :] = got[0, c, n]
            ref[c, n, 2 + g.sub : 4 + g.sub, :] = got[1, c, n]


def pack_y(grids, exts, out):
    for tile, (g, ext) in enumerate(zip(grids, exts)):
        lane = lax.broadcasted_iota(jnp.int32, (g.sub, 128), 1)
        total = jnp.zeros((g.sub, 128), jnp.float32)
        for c in range(3):
            for n in range(g.lead):
                i = c * g.lead + n
                plane = ext[2][c, n, :, 0:128]
                if g.ny > 128:
                    plane = jnp.where(lane < 64, plane, ext[2][c, n, :, g.ny - 128 : g.ny])
                total = jnp.where(lane // 4 == i, roll(plane, 4 * i + 2, 1), total)
        out[tile, 0 : g.sub, :] = total


def unpack_y(grids, exts, got):
    for tile, (g, ext) in enumerate(zip(grids, exts)):
        lane = lax.broadcasted_iota(jnp.int32, (g.sub, 128), 1)
        both = jnp.where(lane % 4 < 2, got[0, tile, 0 : g.sub, :], got[1, tile, 0 : g.sub, :])
        for c in range(3):
            for n in range(g.lead):
                i = c * g.lead + n
                ext[2][c, n, :, g.ny : g.ny + 128] = roll(both, -(4 * i + 2), 1)


def couple(fine, coarse, fext, cext):
    fz, cz = fext[0], cext[0]
    nt = fine.ny // 128
    rows = fz.shape[2]
    lane = lax.broadcasted_iota(jnp.int32, (rows, 128), 1)
    clane = lane[0 : coarse.sub]
    last = 1 + fine.sub
    for c in range(3):
        plane = cz[c, 2]
        spread = jnp.concatenate(
            [jnp.take_along_axis(plane, (clane + 128 * t) // 3, axis=1) for t in range(nt)], axis=1
        )
        for n in range(fine.lead):
            bottom = fz[c, n, last : last + 1, :]
            row = spread[n // 3 : n // 3 + 1]
            fz[c, n, last + 1 : last + 2, :] = 2.0 / 3.0 * bottom + 1.0 / 3.0 * row
            fz[c, n, last + 2 : last + 3, :] = 1.0 / 3.0 * bottom + 2.0 / 3.0 * row
        for r in range(coarse.sub):
            f = fz[c, 3 * r] + fz[c, 3 * r + 1] + fz[c, 3 * r + 2]
            f = f + roll(f, -1, 1) + roll(f, -2, 1)
            out = jnp.zeros((rows, 128), jnp.float32)
            for t in range(nt):
                got = jnp.take_along_axis(f[:, 128 * t : 128 * t + 128], (3 * lane) % 128, axis=1)
                out = jnp.where((3 * lane) // 128 == t, got, out)
            out = out * (1.0 / 9.0)
            cz[c, 1, r : r + 1, :] = out[last : last + 1]
            cz[c, 0, r : r + 1, :] = out[last - 3 : last - 2]


def materials(g, zones, tables, out):
    def body(z, carry):
        ids = zones[g.at(z)]
        values = [jnp.zeros(ids.shape, jnp.float32)] * 3
        for member in range(tables[0].shape[0]):
            hit = ids == member
            values = [jnp.where(hit, t[member], v) for t, v in zip(tables, values)]
        out[0, z] = DT * values[0]
        out[1, z] = DT * values[1]
        out[2, z] = DT * values[2]
        return carry

    lax.fori_loop(0, g.lead, body, 0)


def velocity_update(g, sext, vext, mats, velocity):
    allc = (0, 1, 2)

    def body(z, carry):
        b = mats[0, z]
        force = (
            diff(g, 1, sext, 0, z, True) + diff(g, 2, sext, 1, z, False) + diff(g, 0, sext, 1, z, False),
            diff(g, 1, sext, 1, z, False) + diff(g, 2, sext, 0, z, True) + diff(g, 0, sext, 2, z, False),
            diff(g, 1, sext, 2, z, False) + diff(g, 2, sext, 2, z, False) + diff(g, 0, sext, 0, z, True),
        )
        new = [velocity[c, g.at(z)] + b * force[c] for c in range(3)]
        for c in range(3):
            velocity[c, g.at(z)] = new[c]
        put_ext(g, vext, (allc, allc, allc), z, new)
        return carry

    lax.fori_loop(0, g.lead, body, 0)


def stress_update(g, vext, sext, mats, stress, iwan, last):

    def body(z, carry):
        lame, shear = mats[1, z], mats[2, z]
        exx = diff(g, 1, vext, 0, z, False)
        eyy = diff(g, 2, vext, 1, z, False)
        ezz = diff(g, 0, vext, 2, z, False)
        exy = diff(g, 1, vext, 1, z, True) + diff(g, 2, vext, 0, z, True)
        exz = diff(g, 1, vext, 2, z, True) + diff(g, 0, vext, 0, z, True)
        eyz = diff(g, 2, vext, 2, z, True) + diff(g, 0, vext, 1, z, True)
        dilation = exx + eyy + ezz
        old = [stress[c, g.at(z)] for c in range(6)]
        volume = lame * dilation
        twice = 2.0 * shear
        shears = [shear * exy, shear * exz, shear * eyz]
        new = [old[c] + volume + twice * e for c, e in enumerate((exx, eyy, ezz))]
        new += [old[3 + c] + shears[c] for c in range(3)]
        if iwan is not None:
            states, plastic, share, radius, surfaces = iwan
            third = dilation * (1.0 / 3.0)
            total = share[0]
            for k in range(1, surfaces):
                total = total + share[k]
            scale = 1.0 / jnp.full(dilation.shape, total, jnp.float32)
            dd = [scale * (twice * (e - third)) for e in (exx, eyy, ezz)]
            dd += [scale * s for s in shears]
            sums = None
            for k in range(surfaces):
                t = [states[k, c, z] + share[k] * dd[c] for c in range(6)]
                j2 = 0.5 * (t[0] * t[0] + t[1] * t[1] + t[2] * t[2]) + (
                    t[3] * t[3] + t[4] * t[4] + t[5] * t[5]
                )
                factor = jnp.minimum(1.0, radius[k] * lax.rsqrt(j2))
                t = [factor * x for x in t]
                if not last:
                    for c in range(6):
                        states[k, c, z] = t[c]
                sums = t if sums is None else [a + b for a, b in zip(sums, t)]
            mean = (old[0] + old[1] + old[2]) * (1.0 / 3.0) + (lame + twice * (1.0 / 3.0)) * dilation
            active = plastic[z] == 1
            yielded = [mean + sums[c] for c in range(3)] + sums[3:]
            new = [jnp.where(active, a, b) for a, b in zip(yielded, new)]
        for c in range(6):
            stress[c, g.at(z)] = new[c]
        if not last:
            put_ext(g, sext, (Z_PARTS, X_PARTS, Y_PARTS), z, new)
        return carry

    lax.fori_loop(0, g.lead, body, 0)


def kernel(counts, fine, coarse, surfaces, *refs):
    tables, share, radius = refs[8:11], refs[11], refs[12]
    outs = refs[13:17]
    (fv, fs, cv, cs, st, fzo, czo, plastic) = refs[17:25]
    fmat, cmat = refs[25:27]
    fsx, csx, fvx, cvx = refs[27:30], refs[30:33], refs[33:36], refs[36:39]
    fsub, csub, ysend, fsub_got, csub_got, ygot = refs[39:45]
    in_sem, out_sem, send_sem, recv_sem = refs[45:49]
    grids = (fine, coarse)

    place = [lax.axis_index(a) for a in AXES]
    exists = lambda a, side: (place[a] > 0) if side == 0 else (place[a] < counts[a] - 1)
    peer = lambda a, side: {AXES[a]: place[a] + (1 if side else -1)}

    loads = [
        pltpu.make_async_copy(src, dst, in_sem.at[i])
        for i, (src, dst) in enumerate(zip(refs[:8], refs[17:25]))
    ]
    for i in (1, 3, 0, 2, 5, 6, 7, 4):
        loads[i].start()

    def lead_face(g, ref, side, halo):
        low = 0 if halo else 2
        high = 2 + g.lead if halo else g.lead
        up = side if not g.flipped else 1 - side
        return ref.at[:, pl.ds(high if up else low, 2)]

    barrier = pltpu.get_barrier_semaphore()
    for a in range(3):
        for side in range(2):

            @pl.when(exists(a, side))
            def _():
                pl.semaphore_signal(barrier, inc=1, device_id=peer(a, side), device_id_type=MESH)

            @pl.when(jnp.logical_not(exists(a, side)))
            def _():
                if a == 2:
                    for e in range(2 * STEPS):
                        ygot[e, side] = jnp.zeros(ygot.shape[2:], jnp.float32)
                    return
                for g, ext, sub in (
                    (fine, fsx, fsub_got), (fine, fvx, None), (coarse, csx, csub_got), (coarse, cvx, None)
                ):
                    if a == g.lead_axis:
                        up = side if not g.flipped else 1 - side
                        at = 2 + g.lead if up else 0
                        for c in range(3):
                            for l in range(2):
                                ext[a][c, at + l] = jnp.zeros((g.sub, g.ny), jnp.float32)
                    elif sub is not None:
                        for e in range(2 * STEPS):
                            sub[e, side] = jnp.zeros(sub.shape[2:], jnp.float32)

    def copies(e, a, side):
        fext, cext = (fsx, csx) if e % 2 == 0 else (fvx, cvx)
        other = 1 - side
        if a == 2:
            pairs = [(ysend.at[e], ygot.at[e, other])]
        else:
            pairs = []
            for g, ext, sub, got in ((fine, fext, fsub, fsub_got), (coarse, cext, csub, csub_got)):
                if a == g.lead_axis:
                    pairs.append((lead_face(g, ext[a], side, False), lead_face(g, ext[a], other, True)))
                else:
                    pairs.append((sub.at[e, side], got.at[e, other]))
        return [
            pltpu.make_async_remote_copy(
                src_ref=src,
                dst_ref=dst,
                send_sem=send_sem.at[e, a, side, i],
                recv_sem=recv_sem.at[e, a, other, i],
                device_id=peer(a, side),
                device_id_type=MESH,
            )
            for i, (src, dst) in enumerate(pairs)
        ]

    def start(e, a):
        for side in range(2):

            @pl.when(exists(a, side))
            def _():
                for copy in copies(e, a, side):
                    copy.start()

    def arrive(e, a):
        for side in range(2):

            @pl.when(exists(a, side))
            def _():
                for copy in copies(e, a, 1 - side):
                    copy.wait_recv()

    def left(e):
        for a in range(3):
            for side in range(2):

                @pl.when(exists(a, side))
                def _():
                    for copy in copies(e, a, side):
                        copy.wait_send()

    parts = (Z_PARTS, X_PARTS, Y_PARTS)
    loads[1].wait()
    loads[3].wait()
    for g, s, ext in ((fine, fs, fsx), (coarse, cs, csx)):
        for n in range(g.lead):
            put_ext(g, ext, parts, n, [s[c, g.at(n)] for c in range(6)])

    at_interface = place[0] == counts[0] - 1
    for e in range(2 * STEPS):
        fext, cext = exts = (fsx, csx) if e % 2 == 0 else (fvx, cvx)
        pack_sub(coarse, cext, csub.at[e])
        if e == 0:
            neighbours = sum(
                exists(a, side).astype(jnp.int32) for a in range(3) for side in range(2)
            )
            pl.semaphore_wait(barrier, neighbours)
        start(e, 1)
        pack_sub(fine, fext, fsub.at[e])
        start(e, 0)
        pack_y(grids, exts, ysend.at[e])
        start(e, 2)
        if e == 0:
            loads[5].wait()
            loads[6].wait()
            materials(fine, fzo, tables, fmat)
            materials(coarse, czo, tables, cmat)
            loads[0].wait()
            loads[2].wait()
        arrive(e, 0)
        unpack_sub(fine, fext, fsub_got.at[e])

        @pl.when(at_interface)
        def _():
            couple(fine, coarse, fext, cext)

        arrive(e, 1)
        unpack_sub(coarse, cext, csub_got.at[e])
        arrive(e, 2)
        unpack_y(grids, exts, ygot.at[e])
        left(e)
        last = e >= 2 * STEPS - 2
        if e % 2 == 0:
            velocity_update(fine, fsx, fvx, fmat, fv)
            velocity_update(coarse, csx, cvx, cmat, cv)
            if last:
                stores = [
                    pltpu.make_async_copy(fv, outs[0], out_sem.at[0]),
                    pltpu.make_async_copy(cv, outs[2], out_sem.at[1]),
                ]
                for s in stores:
                    s.start()
        else:
            if e == 1:
                loads[7].wait()
                loads[4].wait()
            stress_update(
                fine, fvx, fsx, fmat, fs, (st, plastic, share, radius, surfaces), last
            )
            stress_update(coarse, cvx, csx, cmat, cs, None, last)
    tail = [
        pltpu.make_async_copy(fs, outs[1], out_sem.at[2]),
        pltpu.make_async_copy(cs, outs[3], out_sem.at[3]),
    ]
    for s in tail:
        s.start()
    for s in stores + tail:
        s.wait()


def swap(x):
    return jnp.swapaxes(x, -3, -2)


def per_device(counts, *args):
    args = [swap(x) if i in (0, 1, 4, 5, 7) else x for i, x in enumerate(args)]
    fv, fs, cv, cs, st = args[:5]
    fine = Grid(fv.shape[1:], 1.0, False, 1)
    coarse = Grid(cv.shape[1:], 3.0, True, 0)
    f32 = jnp.float32

    def exts(g):
        lead = pltpu.VMEM((3, g.lead + 4, g.sub, g.ny), f32)
        sub = pltpu.VMEM((3, g.lead, -(-(g.sub + 4) // 8) * 8, g.ny), f32)
        return [
            lead if g.lead_axis == 0 else sub,
            lead if g.lead_axis == 1 else sub,
            pltpu.VMEM((3, g.lead, g.sub, g.ny + 128), f32),
        ]

    phases = 2 * STEPS
    subs = [pltpu.VMEM((phases, 2, 3, g.lead, 2, g.ny), f32) for g in (fine, coarse)]
    scratch = [pltpu.VMEM(a.shape, a.dtype) for a in args[:8]]
    scratch += [pltpu.VMEM((3, g.lead, g.sub, g.ny), f32) for g in (fine, coarse)]
    scratch += exts(fine) + exts(coarse) + exts(fine) + exts(coarse)
    scratch += subs + [pltpu.VMEM((phases, 2, 8, 128), f32)]
    scratch += subs + [pltpu.VMEM((phases, 2, 2, 8, 128), f32)]
    scratch += [
        pltpu.SemaphoreType.DMA((8,)),
        pltpu.SemaphoreType.DMA((4,)),
        pltpu.SemaphoreType.DMA((phases, 3, 2, 2)),
        pltpu.SemaphoreType.DMA((phases, 3, 2, 2)),
    ]
    anywhere = pl.BlockSpec(memory_space=pl.ANY)
    scalars = pl.BlockSpec(memory_space=pltpu.SMEM)
    out = pl.pallas_call(
        lambda *refs: kernel(counts, fine, coarse, st.shape[0], *refs),
        name="waves",
        out_shape=[jax.ShapeDtypeStruct(a.shape, a.dtype) for a in (fv, fs, cv, cs)],
        in_specs=[anywhere] * 8 + [scalars] * 5,
        out_specs=[anywhere] * 4,
        scratch_shapes=scratch,
        compiler_params=pltpu.CompilerParams(collective_id=0, has_side_effects=True),
    )(*args)
    return swap(out[0]), swap(out[1]), out[2], out[3]


def solution(mesh):
    field = P(None, *AXES)
    cells = P(*AXES)
    counts = tuple(mesh.shape[a] for a in AXES)
    return jax.shard_map(
        lambda *args: per_device(counts, *args),
        mesh=mesh,
        in_specs=(field,) * 4 + (P(None, None, *AXES),) + (cells,) * 3 + (P(),) * 5,
        out_specs=(field,) * 4,
        check_vma=False,
    )
```

time: 40.6 us -> 31.4 us (0.77)
  local copies, waits for them, and re-layouts: 15.6 us -> 5.79 us
  Pallas kernels: 23.9 us -> 24.7 us
    unnamed x7 -> x4, local copies, waits for them, and re-layouts: 12.4 us -> 5.79 us
    pallas_call x2 -> x0, local copies, waits for them, and re-layouts: 3.29 us -> none  [per_device(): pl.pallas_call(lambda *refs: kernel(counts, fine, coarse, st.shape[0], *r...]
    pallas_call x1, Pallas kernels: 23.9 us -> 24.7 us  [per_device(): pl.pallas_call(lambda *refs: kernel(counts, fine, coarse, st.shape[0], *r...]
where the time goes in v1:
time: 31.4 us; the launch traced here: 31.1 us
  Pallas kernels  24.7 us (79%)
  local copies, waits for them, and re-layouts  5.79 us (18%)
  between operations  0.65 us (2%)
    pallas_call x1, Pallas kernels, per_device(): pl.pallas_call(lambda *refs: kernel(counts, fine, coarse, st.shape[0], *r...  24.7 us
    unnamed x4, local copies, waits for them, and re-layouts  5.79 us

profile of v1, /device:TPU:0, one launch (start us, length us, event | category | flops | bytes accessed | tf_op | source)
XLA Modules:
  0.0 31.1 jit_solution(7829071415281011728)
XLA Ops:
  0.6 24.7 %waves.1 = (f32[3,6,4,384]{3,2,1,0:T(4,128)}, f32[6,6,4,384]{3,2,1,0:T(4,128)}, f32[3,2,2,128]{3,2,1,0:T(2,128)}, f32[6,2,2,128]{3,2,1,0:T(2,128)}) custom-call(f32[3,6,4,384]{3,2,1,0:T(4,128)} %bitcast.11, f32[6,6,4,384]{3,2,1,0:T(4,128)} %bitcast.8, f32[3,2,2,128]{3,2,1,0:T(2,128)} %refs_2_.1, f32[6,2,2,128]{3,2,1,0:T(2,128)} %refs_3_.1, ...), custom_call_target="tpu_custom_call" | custom-call | tf_op jit(solution)/shard_map/waves/pallas_call | solution.py:420
  25.3 1.6 %copy.21 = f32[3,4,6,384]{3,1,2,0:T(4,128)} copy(f32[3,4,6,384]{3,1,2,0:T(4,128)} %bitcast.10) | data formatting | bytes 221184
  26.9 1.6 %copy.22 = f32[6,4,6,384]{3,1,2,0:T(4,128)} copy(f32[6,4,6,384]{3,1,2,0:T(4,128)} %bitcast.9) | data formatting | bytes 442368
  28.5 1.3 %copy.23 = f32[3,2,2,128]{3,2,1,0:T(2,128)} copy(f32[3,2,2,128]{3,2,1,0:T(2,128)} %get-tuple-element.18) | data formatting | bytes 12288
  29.8 1.3 %copy.24 = f32[6,2,2,128]{3,2,1,0:T(2,128)} copy(f32[6,2,2,128]{3,2,1,0:T(2,128)} %get-tuple-element.19) | data formatting | bytes 24576

commit v2 on v1

--- a/solution.py
+++ b/solution.py
@@ -140,10 +140,22 @@
     lax.fori_loop(0, g.lead, body, 0)
 
 
-def velocity_update(g, sext, vext, mats, velocity):
+class Planes:
+    def __init__(self, g, kind):
+        self.kind, self.lead = kind, g.lead
+        self.count = {"all": g.lead, "inner": g.lead - 4, "outer": 4}[kind]
+
+    def __call__(self, i):
+        if self.kind == "outer":
+            return i + (i // 2) * (self.lead - 4)
+        return i + 2 if self.kind == "inner" else i
+
+
+def velocity_update(g, sext, vext, mats, velocity, out, planes):
     allc = (0, 1, 2)
 
-    def body(z, carry):
+    def body(i, carry):
+        z = planes(i)
         b = mats[0, z]
         force = (
             diff(g, 1, sext, 0, z, True) + diff(g, 2, sext, 1, z, False) + diff(g, 0, sext, 1, z, False),
@@ -152,16 +164,17 @@
         )
         new = [velocity[c, g.at(z)] + b * force[c] for c in range(3)]
         for c in range(3):
-            velocity[c, g.at(z)] = new[c]
+            out[c, g.at(z)] = new[c]
         put_ext(g, vext, (allc, allc, allc), z, new)
         return carry
 
-    lax.fori_loop(0, g.lead, body, 0)
-
-
-def stress_update(g, vext, sext, mats, stress, iwan, last):
-
-    def body(z, carry):
+    lax.fori_loop(0, planes.count, body, 0)
+
+
+def stress_update(g, vext, sext, mats, stress, out, iwan, last, planes):
+
+    def body(i, carry):
+        z = planes(i)
         lame, shear = mats[1, z], mats[2, z]
         exx = diff(g, 1, vext, 0, z, False)
         eyy = diff(g, 2, vext, 1, z, False)
@@ -202,22 +215,22 @@
             yielded = [mean + sums[c] for c in range(3)] + sums[3:]
             new = [jnp.where(active, a, b) for a, b in zip(yielded, new)]
         for c in range(6):
-            stress[c, g.at(z)] = new[c]
+            out[c, g.at(z)] = new[c]
         if not last:
             put_ext(g, sext, (Z_PARTS, X_PARTS, Y_PARTS), z, new)
         return carry
 
-    lax.fori_loop(0, g.lead, body, 0)
+    lax.fori_loop(0, planes.count, body, 0)
 
 
 def kernel(counts, fine, coarse, surfaces, *refs):
-    tables, share, radius = refs[8:11], refs[11], refs[12]
+    tables, share, radius = refs[48:51], refs[51], refs[52]
     outs = refs[13:17]
     (fv, fs, cv, cs, st, fzo, czo, plastic) = refs[17:25]
     fmat, cmat = refs[25:27]
     fsx, csx, fvx, cvx = refs[27:30], refs[30:33], refs[33:36], refs[36:39]
     fsub, csub, ysend, fsub_got, csub_got, ygot = refs[39:45]
-    in_sem, out_sem, send_sem, recv_sem = refs[45:49]
+    in_sem, send_sem, recv_sem = refs[45:48]
     grids = (fine, coarse)
 
     place = [lax.axis_index(a) for a in AXES]
@@ -228,7 +241,12 @@
         pltpu.make_async_copy(src, dst, in_sem.at[i])
         for i, (src, dst) in enumerate(zip(refs[:8], refs[17:25]))
     ]
-    for i in (1, 3, 0, 2, 5, 6, 7, 4):
+    scalars = [
+        pltpu.make_async_copy(src, dst, in_sem.at[8 + i])
+        for i, (src, dst) in enumerate(zip(refs[8:13], refs[48:53]))
+    ]
+
+    for i in (1, 3):
         loads[i].start()
 
     def lead_face(g, ref, side, halo):
@@ -263,6 +281,9 @@
                     elif sub is not None:
                         for e in range(2 * STEPS):
                             sub[e, side] = jnp.zeros(sub.shape[2:], jnp.float32)
+
+    for copy in [loads[i] for i in (0, 2, 5, 6)] + scalars + [loads[7], loads[4]]:
+        copy.start()
 
     def copies(e, a, side):
         fext, cext = (fsx, csx) if e % 2 == 0 else (fvx, cvx)
@@ -337,6 +358,8 @@
         if e == 0:
             loads[5].wait()
             loads[6].wait()
+            for copy in scalars:
+                copy.wait()
             materials(fine, fzo, tables, fmat)
             materials(coarse, czo, tables, cmat)
             loads[0].wait()
@@ -348,42 +371,43 @@
         def _():
             couple(fine, coarse, fext, cext)
 
+        arrive(e, 2)
+        unpack_y(grids, exts, ygot.at[e])
+        if e:
+            left(e - 1)
+        last = e >= 2 * STEPS - 2
+        if e == 1:
+            loads[7].wait()
+            loads[4].wait()
+
+        def update(planes):
+            if e % 2 == 0:
+                velocity_update(fine, fsx, fvx, fmat, fv, outs[0] if last else fv, planes)
+            else:
+                iwan = (st, plastic, share, radius, surfaces)
+                stress_update(fine, fvx, fsx, fmat, fs, outs[1] if last else fs, iwan, last, planes)
+
+        update(Planes(fine, "inner"))
         arrive(e, 1)
         unpack_sub(coarse, cext, csub_got.at[e])
-        arrive(e, 2)
-        unpack_y(grids, exts, ygot.at[e])
-        left(e)
-        last = e >= 2 * STEPS - 2
+        update(Planes(fine, "outer"))
         if e % 2 == 0:
-            velocity_update(fine, fsx, fvx, fmat, fv)
-            velocity_update(coarse, csx, cvx, cmat, cv)
-            if last:
-                stores = [
-                    pltpu.make_async_copy(fv, outs[0], out_sem.at[0]),
-                    pltpu.make_async_copy(cv, outs[2], out_sem.at[1]),
-                ]
-                for s in stores:
-                    s.start()
+            velocity_update(coarse, csx, cvx, cmat, cv, outs[2] if last else cv, Planes(coarse, "all"))
         else:
-            if e == 1:
-                loads[7].wait()
-                loads[4].wait()
-            stress_update(
-                fine, fvx, fsx, fmat, fs, (st, plastic, share, radius, surfaces), last
-            )
-            stress_update(coarse, cvx, csx, cmat, cs, None, last)
-    tail = [
-        pltpu.make_async_copy(fs, outs[1], out_sem.at[2]),
-        pltpu.make_async_copy(cs, outs[3], out_sem.at[3]),
-    ]
-    for s in tail:
-        s.start()
-    for s in stores + tail:
-        s.wait()
+            stress_update(coarse, cvx, csx, cmat, cs, outs[3] if last else cs, None, last, Planes(coarse, "all"))
+    left(2 * STEPS - 1)
 
 
 def swap(x):
     return jnp.swapaxes(x, -3, -2)
+
+
+def hand_over(*refs):
+    copies = [pltpu.make_async_copy(refs[i], refs[4 + i], refs[8].at[i]) for i in range(4)]
+    for copy in copies:
+        copy.start()
+    for copy in copies:
+        copy.wait()
 
 
 def per_device(counts, *args):
@@ -410,22 +434,32 @@
     scratch += subs + [pltpu.VMEM((phases, 2, 8, 128), f32)]
     scratch += subs + [pltpu.VMEM((phases, 2, 2, 8, 128), f32)]
     scratch += [
-        pltpu.SemaphoreType.DMA((8,)),
-        pltpu.SemaphoreType.DMA((4,)),
+        pltpu.SemaphoreType.DMA((13,)),
         pltpu.SemaphoreType.DMA((phases, 3, 2, 2)),
         pltpu.SemaphoreType.DMA((phases, 3, 2, 2)),
     ]
+    scratch += [pltpu.SMEM(a.shape, a.dtype) for a in args[8:]]
     anywhere = pl.BlockSpec(memory_space=pl.ANY)
-    scalars = pl.BlockSpec(memory_space=pltpu.SMEM)
     out = pl.pallas_call(
         lambda *refs: kernel(counts, fine, coarse, st.shape[0], *refs),
         name="waves",
+        out_shape=[pltpu.VMEM(a.shape, a.dtype) for a in (fv, fs, cv, cs)],
+        in_specs=[pl.BlockSpec(memory_space=pltpu.HBM)] * 13,
+        out_specs=[pl.BlockSpec(memory_space=pltpu.VMEM)] * 4,
+        scratch_shapes=scratch,
+        compiler_params=pltpu.CompilerParams(
+            collective_id=0, has_side_effects=True
+        ),
+    )(*args)
+    out = pl.pallas_call(
+        hand_over,
+        name="results",
         out_shape=[jax.ShapeDtypeStruct(a.shape, a.dtype) for a in (fv, fs, cv, cs)],
-        in_specs=[anywhere] * 8 + [scalars] * 5,
+        in_specs=[anywhere] * 4,
         out_specs=[anywhere] * 4,
-        scratch_shapes=scratch,
-        compiler_params=pltpu.CompilerParams(collective_id=0, has_side_effects=True),
-    )(*args)
+        scratch_shapes=[pltpu.SemaphoreType.DMA((4,))],
+        compiler_params=pltpu.CompilerParams(vmem_limit_bytes=4 << 20),
+    )(*out)
     return swap(out[0]), swap(out[1]), out[2], out[3]
 
 

time: 31.4 us -> 24.3 us (0.77)
  local copies, waits for them, and re-layouts: 5.79 us -> 0 us
  Pallas kernels: 24.7 us -> 23.5 us
    unnamed x4 -> x0, local copies, waits for them, and re-layouts: 5.79 us -> none
    pallas_call x1, Pallas kernels: 24.7 us -> 22.7 us  [per_device(): pl.pallas_call(lambda *refs: kernel(counts, fine, coarse, st.shape[0], *r...]
    pallas_call x0 -> x1, Pallas kernels: none -> 0.76 us  [per_device(): pl.pallas_call(hand_over, name='results', out_shape=[jax.ShapeDtypeStruct...]
where the time goes in v2:
time: 24.3 us; the launch traced here: 24.2 us
  Pallas kernels  23.5 us (97%)
  between operations  0.64 us (3%)
    pallas_call x1, Pallas kernels, per_device(): pl.pallas_call(lambda *refs: kernel(counts, fine, coarse, st.shape[0], *r...  22.7 us
    pallas_call x1, Pallas kernels, per_device(): pl.pallas_call(hand_over, name='results', out_shape=[jax.ShapeDtypeStruct...  0.76 us

profile of v2, /device:TPU:0, one launch (start us, length us, event | category | flops | bytes accessed | tf_op | source)
XLA Modules:
  0.0 24.2 jit_solution(12244256704537622126)
XLA Ops:
  0.6 22.7 %waves.1 = (f32[3,6,4,384]{3,2,1,0:T(4,128)S(1)}, f32[6,6,4,384]{3,2,1,0:T(4,128)S(1)}, f32[3,2,2,128]{3,2,1,0:T(2,128)S(1)}, f32[6,2,2,128]{3,2,1,0:T(2,128)S(1)}) custom-call(f32[3,6,4,384]{3,2,1,0:T(4,128)} %bitcast.9, f32[6,6,4,384]{3,2,1,0:T(4,128)} %bitcast.8, f32[3,2,2,128]{3,2,1,0:T(2,128)} %refs_2_.1, f32[6,2,2,128]{3,2,1,0:T(2,128)} %refs_3_.1, ...), custom_call_target="tpu_custom_call" | custom-call | tf_op jit(solution)/shard_map/waves/pallas_call | solution.py:443
  23.4 0.8 %results.1 = (f32[3,6,4,384]{3,2,1,0:T(4,128)}, f32[6,6,4,384]{3,2,1,0:T(4,128)}, f32[3,2,2,128]{3,2,1,0:T(2,128)}, f32[6,2,2,128]{3,2,1,0:T(2,128)}) custom-call(f32[3,6,4,384]{3,2,1,0:T(4,128)S(1)} %get-tuple-element.12.refs_0_, f32[6,6,4,384]{3,2,1,0:T(4,128)S(1)} %get-tuple-element.13.refs_1_, f32[3,2,2,128]{3,2,1,0:T(2,128)S(1)} %get-tuple-element.14.refs_2_, ...), custom_call_target="tpu_custom_call" | custom-call | tf_op jit(solution)/shard_map/results/pallas_call | solution.py:454
